TPU v7x, 32 devices: a whole 2x2x4 slice. The times are simulated.
32 devices in a mesh: grp: 2 (over core), tile: 16 (over z, y, x).
Axes of the slice: x: 2, y: 2, z: 4, core: 2. Of those that a mesh axis runs over, the one named last changes fastest.
Arguments:
- attn_input: bfloat16 [2048, 4096], P(('grp', 'tile')), may hold values from -9 to 9
- mlp_input: bfloat16 [2048, 4096], P(('grp', 'tile')), may hold values from -9 to 9
Outputs:
- hess_attn: float32 [16, 1024, 1024], P('tile', 'grp')
- hess_mlp: float32 [16, 1024, 1024], P('tile', 'grp')
All inputs are finite; a program needn't handle non-finite values.
Results may differ from a plain program's by a relative error of at most 0.0003.
Values may be sent and summed in bfloat16 or wider, within the bound.
A program may use at most 192 MiB of HBM per device.

v0:
```python
import jax
import jax.numpy as jnp
from jax import lax
from jax.sharding import PartitionSpec as P

ROWB = 4
TOKB = 32


def tile_first(inputs, tile_count):
    tok_rows, feat_width = inputs.shape
    col_blocks = tile_count // ROWB
    row_width = feat_width // ROWB
    col_width = feat_width // col_blocks

    def accumulate(turn_idx, partial_value):
        tok_block = lax.dynamic_slice_in_dim(inputs, turn_idx * TOKB, TOKB, 0)
        row_parts = tok_block.reshape(TOKB, ROWB, row_width).transpose(1, 0, 2)
        row_send = jnp.repeat(row_parts, col_blocks, axis=0)
        col_parts = tok_block.reshape(TOKB, col_blocks, col_width).transpose(1, 0, 2)
        col_send = jnp.tile(col_parts, (ROWB, 1, 1))
        rows_in, cols_in = (
            lax.all_to_all(row_send, "tile", split_axis=0, concat_axis=0, tiled=True),
            lax.all_to_all(col_send, "tile", split_axis=0, concat_axis=0, tiled=True),
        )
        rows_flat = rows_in.reshape(tile_count * TOKB, row_width)
        cols_flat = cols_in.reshape(tile_count * TOKB, col_width)
        return partial_value + lax.dot_general(
            rows_flat, cols_flat, (((0,), (0,)), ((), ())), preferred_element_type=jnp.float32
        )

    partial_value = lax.fori_loop(
        0, tok_rows // TOKB, accumulate, jnp.zeros((row_width, col_width), jnp.float32)
    )
    shares = lax.psum_scatter(partial_value, "grp", scatter_dimension=0, tiled=True)
    return shares[None]


def hessian_share(inputs):
    tile_count = lax.axis_size("tile")
    group_count = lax.axis_size("grp")
    norm_factor = 2.0 / (inputs.shape[0] * tile_count * group_count)
    shares = tile_first(inputs, tile_count)
    return shares * norm_factor


def body(attn_input, mlp_input):
    return (hessian_share(attn_input), hessian_share(mlp_input))


def solution(mesh):
    in_specs = (P(("grp", "tile"), None), P(("grp", "tile"), None))
    out_specs = (P("tile", "grp", None), P("tile", "grp", None))
    return jax.shard_map(body, mesh=mesh, in_specs=in_specs, out_specs=out_specs, check_vma=False)
```

profile of v0, /device:TPU:2, one launch (start us, length us, event | category | flops | bytes accessed | tf_op | source)
XLA Modules:
  0.0 289.9 jit_solution(9503920627443665375)
XLA Ops:
  7.2 0.0 reduce-scatter.5.cloned.1.call-start
  7.2 130.9 %while.29 = (s32[]{:T(128)}, f32[1024,1024]{1,0:T(8,128)}, bf16[64,4096]{1,0:T(8,128)(2,1)}, s32[]{:T(128)}, s32[]{:T(128)}, /*index=5*/s32[]{:T(128)}, s32[]{:T(128)}) while((s32[]{:T(128)}, f32[1024,1024]{1,0:T(8,128)}, bf16[64,4096]{1,0:T(8,128)(2,1)}, s32[]{:T(128)}, s32[]{:T(128)}, /*index=5*/s32[]{:T(128)}, s32[]{:T(128)}) %tuple.66), condition=%wide.region_4.0_spmd.clone, body=%wide.region_3.0_spmd.clone.sunk | while | flops 1075838976 | bytes 19923112 | solution.py:32
  7.2 1.0 constant_dynamic-slice_fusion.5
  8.2 0.2 reshape.65
  8.4 0.1 copy.11
  8.5 0.1 tile.49
  8.6 32.1 %all_to_all.45 = bf16[16,32,1024]{2,1,0:T(8,128)(2,1)S(1)} all-to-all(bf16[16,32,1024]{2,1,0:T(8,128)(2,1)S(1)} %bitcast.42), channel_id=1, replica_groups=mesh['grp'=2,'tile'=16] {'tile'}, dimensions={0} | all-to-all | bytes 2097152 | tf_op jit(solution)/shard_map/while/body/eval_jaxpr/all_to_all | solution.py:24
  40.7 1.1 broadcast_in_dim.21
  41.8 5.3 %all-to-all-start.2 = ((bf16[16,32,1024]{2,1,0:T(8,128)(2,1)}), bf16[16,32,1024]{2,1,0:T(8,128)(2,1)S(1)}, u32[]{:S(2)}, u32[]{:S(2)}) async-start(bf16[16,32,1024]{2,1,0:T(8,128)(2,1)} %bitcast.40), calls=%async_computation.2 | async-start | bytes 2097152 | tf_op jit(solution)/shard_map/while/body/eval_jaxpr/all_to_all | solution.py:23
  47.1 22.3 %all-to-all-done.2 = bf16[16,32,1024]{2,1,0:T(8,128)(2,1)S(1)} async-done(((bf16[16,32,1024]{2,1,0:T(8,128)(2,1)}), bf16[16,32,1024]{2,1,0:T(8,128)(2,1)S(1)}, u32[]{:S(2)}, u32[]{:S(2)}) %all-to-all-start.2) | async-done | bytes 1048608 | tf_op jit(solution)/shard_map/while/body/eval_jaxpr/all_to_all | solution.py:23
  69.4 3.3 %bitcast_add_fusion.5 = f32[1024,1024]{1,0:T(8,128)} fusion(f32[1024,1024]{1,0:T(8,128)} %get-tuple-element.235, bf16[16,32,1024]{2,1,0:T(8,128)(2,1)S(1)} %all-to-all-done.2, bf16[16,32,1024]{2,1,0:T(8,128)(2,1)S(1)} %all_to_all.45, pred[]{:T(512)S(6)} %compare.7), kind=kOutput, calls=%fused_computation.2.clone.1 | convolution fusion | flops 1075838976 | bytes 10485761 | tf_op jit(solution)/shard_map/while/body/eval_jaxpr/dot_general | solution.py:28
  72.7 1.0 constant_dynamic-slice_fusion.5
  73.6 0.2 reshape.65
  73.8 0.1 copy.11
  73.9 0.1 tile.49
  74.0 30.7 %all_to_all.45 = bf16[16,32,1024]{2,1,0:T(8,128)(2,1)S(1)} all-to-all(bf16[16,32,1024]{2,1,0:T(8,128)(2,1)S(1)} %bitcast.42), channel_id=1, replica_groups=mesh['grp'=2,'tile'=16] {'tile'}, dimensions={0} | all-to-all | bytes 2097152 | tf_op jit(solution)/shard_map/while/body/eval_jaxpr/all_to_all | solution.py:24
  104.7 1.1 broadcast_in_dim.21
  105.8 5.3 %all-to-all-start.2 = ((bf16[16,32,1024]{2,1,0:T(8,128)(2,1)}), bf16[16,32,1024]{2,1,0:T(8,128)(2,1)S(1)}, u32[]{:S(2)}, u32[]{:S(2)}) async-start(bf16[16,32,1024]{2,1,0:T(8,128)(2,1)} %bitcast.40), calls=%async_computation.2 | async-start | bytes 2097152 | tf_op jit(solution)/shard_map/while/body/eval_jaxpr/all_to_all | solution.py:23
  111.1 21.6 %all-to-all-done.2 = bf16[16,32,1024]{2,1,0:T(8,128)(2,1)S(1)} async-done(((bf16[16,32,1024]{2,1,0:T(8,128)(2,1)}), bf16[16,32,1024]{2,1,0:T(8,128)(2,1)S(1)}, u32[]{:S(2)}, u32[]{:S(2)}) %all-to-all-start.2) | async-done | bytes 1048608 | tf_op jit(solution)/shard_map/while/body/eval_jaxpr/all_to_all | solution.py:23
  132.7 5.5 %bitcast_add_fusion.5 = f32[1024,1024]{1,0:T(8,128)} fusion(f32[1024,1024]{1,0:T(8,128)} %get-tuple-element.235, bf16[16,32,1024]{2,1,0:T(8,128)(2,1)S(1)} %all-to-all-done.2, bf16[16,32,1024]{2,1,0:T(8,128)(2,1)S(1)} %all_to_all.45, pred[]{:T(512)S(6)} %compare.7), kind=kOutput, calls=%fused_computation.2.clone.1 | convolution fusion | flops 1075838976 | bytes 10485761 | tf_op jit(solution)/shard_map/while/body/eval_jaxpr/dot_general | solution.py:28
  138.2 0.0 copy-start
  138.2 0.0 reduce-scatter.5.cloned.1.call-update
  138.2 0.0 reduce-scatter.3.cloned.1.call-start
  138.2 1.0 copy-done
  139.2 126.8 %while.28 = (s32[]{:T(128)}, f32[1024,1024]{1,0:T(8,128)}, bf16[64,4096]{1,0:T(8,128)(2,1)S(1)}, s32[]{:T(128)}, s32[]{:T(128)}, /*index=5*/s32[]{:T(128)}, s32[]{:T(128)}) while((s32[]{:T(128)}, f32[1024,1024]{1,0:T(8,128)}, bf16[64,4096]{1,0:T(8,128)(2,1)S(1)}, s32[]{:T(128)}, s32[]{:T(128)}, /*index=5*/s32[]{:T(128)}, ...), condition=%wide.region_1.0_spmd.clone, body=%wide.region_0.0_spmd.clone.sunk | while | flops 1075838976 | bytes 19923112 | solution.py:32
  139.2 0.2 reshape.64
  139.4 0.1 copy.10
  139.5 0.1 tile.48
  139.6 30.7 %all_to_all.44 = bf16[16,32,1024]{2,1,0:T(8,128)(2,1)S(1)} all-to-all(bf16[16,32,1024]{2,1,0:T(8,128)(2,1)S(1)} %bitcast.43), channel_id=1, replica_groups=mesh['grp'=2,'tile'=16] {'tile'}, dimensions={0} | all-to-all | bytes 2097152 | tf_op jit(solution)/shard_map/while/body/eval_jaxpr/all_to_all | solution.py:24
  170.3 1.1 broadcast_in_dim.20
  171.4 5.3 %all-to-all-start = ((bf16[16,32,1024]{2,1,0:T(8,128)(2,1)}), bf16[16,32,1024]{2,1,0:T(8,128)(2,1)S(1)}, u32[]{:S(2)}, u32[]{:S(2)}) async-start(bf16[16,32,1024]{2,1,0:T(8,128)(2,1)} %bitcast.34), calls=%async_computation | async-start | bytes 2097152 | tf_op jit(solution)/shard_map/while/body/eval_jaxpr/all_to_all | solution.py:23
  176.7 21.5 %all-to-all-done = bf16[16,32,1024]{2,1,0:T(8,128)(2,1)S(1)} async-done(((bf16[16,32,1024]{2,1,0:T(8,128)(2,1)}), bf16[16,32,1024]{2,1,0:T(8,128)(2,1)S(1)}, u32[]{:S(2)}, u32[]{:S(2)}) %all-to-all-start) | async-done | bytes 1048608 | tf_op jit(solution)/shard_map/while/body/eval_jaxpr/all_to_all | solution.py:23
  198.2 3.2 %bitcast_add_fusion.4 = f32[1024,1024]{1,0:T(8,128)} fusion(f32[1024,1024]{1,0:T(8,128)} %get-tuple-element.214, bf16[16,32,1024]{2,1,0:T(8,128)(2,1)S(1)} %all-to-all-done, bf16[16,32,1024]{2,1,0:T(8,128)(2,1)S(1)} %all_to_all.44, pred[]{:T(512)S(6)} %compare.6), kind=kOutput, calls=%fused_computation.clone.1 | convolution fusion | flops 1075838976 | bytes 10485761 | tf_op jit(solution)/shard_map/while/body/eval_jaxpr/dot_general | solution.py:28
  201.5 0.2 reshape.64
  201.7 0.1 copy.10
  201.8 0.1 tile.48
  201.9 30.7 %all_to_all.44 = bf16[16,32,1024]{2,1,0:T(8,128)(2,1)S(1)} all-to-all(bf16[16,32,1024]{2,1,0:T(8,128)(2,1)S(1)} %bitcast.43), channel_id=1, replica_groups=mesh['grp'=2,'tile'=16] {'tile'}, dimensions={0} | all-to-all | bytes 2097152 | tf_op jit(solution)/shard_map/while/body/eval_jaxpr/all_to_all | solution.py:24
  232.6 1.1 broadcast_in_dim.20
  233.7 5.3 %all-to-all-start = ((bf16[16,32,1024]{2,1,0:T(8,128)(2,1)}), bf16[16,32,1024]{2,1,0:T(8,128)(2,1)S(1)}, u32[]{:S(2)}, u32[]{:S(2)}) async-start(bf16[16,32,1024]{2,1,0:T(8,128)(2,1)} %bitcast.34), calls=%async_computation | async-start | bytes 2097152 | tf_op jit(solution)/shard_map/while/body/eval_jaxpr/all_to_all | solution.py:23
  239.0 21.5 %all-to-all-done = bf16[16,32,1024]{2,1,0:T(8,128)(2,1)S(1)} async-done(((bf16[16,32,1024]{2,1,0:T(8,128)(2,1)}), bf16[16,32,1024]{2,1,0:T(8,128)(2,1)S(1)}, u32[]{:S(2)}, u32[]{:S(2)}) %all-to-all-start) | async-done | bytes 1048608 | tf_op jit(solution)/shard_map/while/body/eval_jaxpr/all_to_all | solution.py:23
  260.5 5.4 %bitcast_add_fusion.4 = f32[1024,1024]{1,0:T(8,128)} fusion(f32[1024,1024]{1,0:T(8,128)} %get-tuple-element.214, bf16[16,32,1024]{2,1,0:T(8,128)(2,1)S(1)} %all-to-all-done, bf16[16,32,1024]{2,1,0:T(8,128)(2,1)S(1)} %all_to_all.44, pred[]{:T(512)S(6)} %compare.6), kind=kOutput, calls=%fused_computation.clone.1 | convolution fusion | flops 1075838976 | bytes 10485761 | tf_op jit(solution)/shard_map/while/body/eval_jaxpr/dot_general | solution.py:28
  266.0 0.0 reduce-scatter.3.cloned.1.call-update
  266.0 0.0 reduce-scatter.5.cloned.1.call-done
  266.0 3.2 %multiply_bitcast_fusion = f32[1,512,1024]{2,1,0:T(8,128)} fusion(f32[512,1024]{1,0:T(8,128)} %reduce-scatter.5.cloned.1.call-done), kind=kLoop, calls=%fused_computation.4 | loop fusion | flops 524288 | bytes 4194304 | tf_op jit(solution)/shard_map/mul | solution.py:44
  269.2 10.6 %reduce-scatter.3.cloned.1.call-done = f32[512,1024]{1,0:T(8,128)} async-done(((f32[1024,1024]{1,0:T(8,128)}), f32[512,1024]{1,0:T(8,128)}) %reduce-scatter.3.cloned.1.call-update) | async-done | bytes 2097168 | tf_op jit(solution)/shard_map/reduce_scatter | solution.py:35
  279.9 3.2 %multiply_bitcast_fusion.1 = f32[1,512,1024]{2,1,0:T(8,128)} fusion(f32[512,1024]{1,0:T(8,128)} %reduce-scatter.3.cloned.1.call-done), kind=kLoop, calls=%fused_computation.5 | loop fusion | flops 524288 | bytes 4194304 | tf_op jit(solution)/shard_map/mul | solution.py:44
  (4 shorter events, 0.0 us)
Async XLA Ops:
  7.2 258.8 %reduce-scatter.5.cloned.1.call-start = ((), (), s32[]{:S(2)}) async-start(), calls=%async_computation.7 | async-start | bytes 6291456 | tf_op jit(solution)/shard_map/reduce_scatter | solution.py:35
  41.8 27.6 %all-to-all-start.2 = ((bf16[16,32,1024]{2,1,0:T(8,128)(2,1)}), bf16[16,32,1024]{2,1,0:T(8,128)(2,1)S(1)}, u32[]{:S(2)}, u32[]{:S(2)}) async-start(bf16[16,32,1024]{2,1,0:T(8,128)(2,1)} %bitcast.40), calls=%async_computation.2 | async-start | bytes 2097152 | tf_op jit(solution)/shard_map/while/body/eval_jaxpr/all_to_all | solution.py:23
  105.8 26.9 %all-to-all-start.2 = ((bf16[16,32,1024]{2,1,0:T(8,128)(2,1)}), bf16[16,32,1024]{2,1,0:T(8,128)(2,1)S(1)}, u32[]{:S(2)}, u32[]{:S(2)}) async-start(bf16[16,32,1024]{2,1,0:T(8,128)(2,1)} %bitcast.40), calls=%async_computation.2 | async-start | bytes 2097152 | tf_op jit(solution)/shard_map/while/body/eval_jaxpr/all_to_all | solution.py:23
  138.2 1.0 copy-start
  138.2 141.7 %reduce-scatter.3.cloned.1.call-start = ((), (), s32[]{:S(2)}) async-start(), calls=%async_computation.6 | async-start | bytes 6291456 | tf_op jit(solution)/shard_map/reduce_scatter | solution.py:35
  171.4 26.8 %all-to-all-start = ((bf16[16,32,1024]{2,1,0:T(8,128)(2,1)}), bf16[16,32,1024]{2,1,0:T(8,128)(2,1)S(1)}, u32[]{:S(2)}, u32[]{:S(2)}) async-start(bf16[16,32,1024]{2,1,0:T(8,128)(2,1)} %bitcast.34), calls=%async_computation | async-start | bytes 2097152 | tf_op jit(solution)/shard_map/while/body/eval_jaxpr/all_to_all | solution.py:23
  233.7 26.8 %all-to-all-start = ((bf16[16,32,1024]{2,1,0:T(8,128)(2,1)}), bf16[16,32,1024]{2,1,0:T(8,128)(2,1)S(1)}, u32[]{:S(2)}, u32[]{:S(2)}) async-start(bf16[16,32,1024]{2,1,0:T(8,128)(2,1)} %bitcast.34), calls=%async_computation | async-start | bytes 2097152 | tf_op jit(solution)/shard_map/while/body/eval_jaxpr/all_to_all | solution.py:23
Sparse Core Ops, SparseCore 0:
  138.3 13.7 reduce-scatter.4
  266.1 13.7 reduce-scatter.2
where the time goes:
time: 292 us; the launch traced here: 290 us
  blocking collectives  124 us (42%)
  waiting for transfers between devices  97.7 us (33%)
  starting transfers between devices  21.2 us (7%)
  matrix products  17.4 us (6%)
  between operations  14.1 us (5%)
  local copies, waits for them, and re-layouts  8.85 us (3%)
  other arithmetic  6.44 us (2%)
    all_to_all x4, blocking collectives, accumulate(): lax.all_to_all(col_send, 'tile', split_axis=0, concat_axis=0, tiled=True)  124 us
    all_to_all x4, waiting for transfers between devices, accumulate(): lax.all_to_all(row_send, 'tile', split_axis=0, concat_axis=0, tiled=True)  87 us
    all_to_all x4, starting transfers between devices, accumulate(): lax.all_to_all(row_send, 'tile', split_axis=0, concat_axis=0, tiled=True)  21.1 us
    dot_general x4, matrix products, accumulate(): lax.dot_general(rows_flat, cols_flat, (((0,), (0,)), ((), ())), preferred...  17.4 us
    reduce_scatter x2, waiting for transfers between devices, tile_first(): lax.psum_scatter(partial_value, 'grp', scatter_dimension=0, tiled=True)  10.7 us
    mul x2, other arithmetic, hessian_share(): return shares * norm_factor  6.44 us
  transfers between devices with their start and end apart: 6, of which 5 were waited for; matrix products, arithmetic and copies ran while one was open for 5% of the time, Pallas kernels for 0%

commit v1 on v0

--- a/solution.py
+++ b/solution.py
@@ -1,10 +1,16 @@
+import functools
+
 import jax
 import jax.numpy as jnp
 from jax import lax
+from jax.experimental import pallas as pl
+from jax.experimental.pallas import tpu as pltpu
 from jax.sharding import PartitionSpec as P
 
 ROWB = 4
 TOKB = 32
+MESH = pl.DeviceIdType.MESH
+LAG = 4
 
 
 def tile_first(inputs, tile_count):
@@ -44,7 +50,229 @@
     return shares * norm_factor
 
 
+def ring_place(member):
+    return member + (member // 2) * (1 - 2 * (member % 2))
+
+
+def piece_of(home, turn):
+    near = home + 1 - 2 * (home % 2)
+    far = (home + 2) % ROWB
+    return jnp.where(turn == 0, home, jnp.where(turn == 1, near, jnp.where(turn == 2, far, ROWB - 1 - home)))
+
+
+def kernel(norm_factor, xa, xm, out_a, out_m, cbuf, dbuf, rbuf, c_recv, d_recv, r_recv, s1_send, dn_send, up_send, d_send, r_send):
+    lines = planes = ROWB
+    g = lax.axis_index("grp")
+    t = lax.axis_index("tile")
+    z, p = t // planes, t % planes
+    tok, _ = xa.shape
+    ct = cbuf.shape[-1]
+    rh = rbuf.shape[-1]
+    xs = (xa, xm)
+    outs = (out_a, out_m)
+    half = pl.ds(pl.multiple_of(g * rh, rh), rh)
+
+    fwd = (ring_place(p) - ring_place(z) + planes) % planes
+    bwd = (planes - fwd) % planes
+    is_root = fwd == 0
+    ring_fwd = ring_place((ring_place(p) + 1) % planes)
+    ring_bwd = ring_place((ring_place(p) + planes - 1) % planes)
+
+    def chip(zz, pp, gg=None):
+        return (g if gg is None else gg, zz * planes + pp)
+
+    barrier = pltpu.get_barrier_semaphore()
+    pl.semaphore_signal(barrier, inc=1, device_id=chip(z, p, 1 - g), device_id_type=MESH)
+    for turn in range(1, planes):
+        pl.semaphore_signal(barrier, inc=1, device_id=chip(z, piece_of(p, turn)), device_id_type=MESH)
+
+    @pl.when(z > 0)
+    def _():
+        pl.semaphore_signal(barrier, inc=1, device_id=chip(z - 1, p), device_id_type=MESH)
+
+    @pl.when(z < lines - 1)
+    def _():
+        pl.semaphore_signal(barrier, inc=1, device_id=chip(z + 1, p), device_id_type=MESH)
+
+    pl.semaphore_wait(barrier, planes + jnp.where(z > 0, 1, 0) + jnp.where(z < lines - 1, 1, 0))
+
+    def s1_copy(a, turn):
+        other = piece_of(p, turn)
+        cols = pl.ds(pl.multiple_of(other * ct, ct), ct)
+        return pltpu.make_async_remote_copy(
+            src_ref=xs[a].at[:, cols], dst_ref=cbuf.at[a, z, p], send_sem=s1_send.at[a, turn - 1],
+            recv_sem=c_recv.at[a, z, p], device_id=chip(z, other), device_id_type=MESH)
+
+    def own_copy(a):
+        cols = pl.ds(pl.multiple_of(p * ct, ct), ct)
+        return pltpu.make_async_copy(xs[a].at[:, cols], cbuf.at[a, z, p], c_recv.at[a, z, p])
+
+    def line_copy(a, slot, piece, down):
+        return pltpu.make_async_remote_copy(
+            src_ref=cbuf.at[a, slot, piece], dst_ref=cbuf.at[a, slot, piece],
+            send_sem=(dn_send if down else up_send).at[a, slot, piece], recv_sem=c_recv.at[a, slot, piece],
+            device_id=chip(z - 1 if down else z + 1, p), device_id_type=MESH)
+
+    def pair_copy(a, slot, piece):
+        return pltpu.make_async_remote_copy(
+            src_ref=cbuf.at[a, slot, piece], dst_ref=dbuf.at[a, slot, piece], send_sem=d_send.at[a, slot, piece],
+            recv_sem=d_recv.at[a, slot, piece], device_id=chip(z, p, 1 - g), device_id_type=MESH)
+
+    def ring_copy(src, a, slot, gg, piece, way):
+        return pltpu.make_async_remote_copy(
+            src_ref=src, dst_ref=rbuf.at[a, slot, gg, piece], send_sem=r_send.at[a, slot, gg, piece],
+            recv_sem=r_recv.at[a, slot, gg, piece],
+            device_id=chip(z, ring_fwd * (1 - way) + ring_bwd * way), device_id_type=MESH)
+
+    def landed(ref, sem):
+        pltpu.make_async_copy(ref, ref, sem).wait()
+
+    for a in range(2):
+        own_copy(a).start()
+        for turn in range(1, planes):
+            s1_copy(a, turn).start()
+    for out in outs:
+        out[...] = jnp.zeros_like(out)
+
+    def root_feed(src, a, slot, gg, piece, turn):
+        @pl.when(is_root)
+        def _():
+            pltpu.make_async_copy(src, rbuf.at[a, slot, gg, piece], r_recv.at[a, slot, gg, piece]).start()
+            ring_copy(src, a, slot, gg, piece, (turn + gg) % 2).start()
+
+    def each_slot(k, action):
+        dist, a, turn = k // (2 * planes), (k // planes) % 2, k % planes
+        high, low = z + dist, z - dist
+
+        @pl.when((k >= 0) & (k < 2 * planes * lines))
+        def _():
+            @pl.when(high < lines)
+            def _():
+                action(a, high, turn, dist, True)
+
+            @pl.when((dist > 0) & (low >= 0))
+            def _():
+                action(a, low, turn, dist, False)
+
+    def col_phase(a, slot, turn, dist, from_high):
+        piece = piece_of(p, turn)
+        landed(cbuf.at[a, slot, piece], c_recv.at[a, slot, piece])
+        if from_high:
+            @pl.when(z > 0)
+            def _():
+                line_copy(a, slot, piece, True).start()
+
+            @pl.when((dist == 0) & (z < lines - 1))
+            def _():
+                line_copy(a, slot, piece, False).start()
+        else:
+            @pl.when(z < lines - 1)
+            def _():
+                line_copy(a, slot, piece, False).start()
+        pair_copy(a, slot, piece).start()
+        root_feed(cbuf.at[a, slot, piece, :, half], a, slot, g, piece, turn)
+
+    def pair_phase(a, slot, turn, dist, from_high):
+        piece = piece_of(p, turn)
+        landed(dbuf.at[a, slot, piece], d_recv.at[a, slot, piece])
+        root_feed(dbuf.at[a, slot, piece, :, half], a, slot, 1 - g, piece, turn)
+
+    def row_phase(a, slot, turn, dist, from_high):
+        piece = piece_of(z, turn)
+        for step in range(2):
+            gg = g if step == 0 else 1 - g
+            landed(rbuf.at[a, slot, gg, piece], r_recv.at[a, slot, gg, piece])
+            way = (turn + gg) % 2
+            span = fwd * (1 - way) + bwd * way
+
+            @pl.when((span > 0) & (span < planes - 1))
+            def _():
+                ring_copy(rbuf.at[a, slot, gg, piece], a, slot, gg, piece, way).start()
+
+        @pl.when(turn == planes - 1)
+        def _():
+            for arr in range(2):
+                @pl.when(a == arr)
+                def _():
+                    total = outs[arr]
+                    for cols, gg in ((cbuf, g), (dbuf, 1 - g)):
+                        total[...] += lax.dot_general(
+                            rbuf[arr, slot, gg].reshape(planes * tok, rh),
+                            cols[arr, slot].reshape(planes * tok, ct),
+                            (((0,), (0,)), ((), ())), preferred_element_type=jnp.float32)
+
+    def step(k, carry):
+        each_slot(k, col_phase)
+        each_slot(k - 1, pair_phase)
+        each_slot(k - LAG, row_phase)
+        return carry
+
+    lax.fori_loop(0, 2 * planes * lines + LAG, step, 0)
+
+    for a in range(2):
+        for turn in range(1, planes):
+            s1_copy(a, turn).wait_send()
+
+    def finish(a, slot, turn, dist, from_high):
+        piece = piece_of(p, turn)
+        if from_high:
+            @pl.when(z > 0)
+            def _():
+                line_copy(a, slot, piece, True).wait_send()
+
+            @pl.when((dist == 0) & (z < lines - 1))
+            def _():
+                line_copy(a, slot, piece, False).wait_send()
+        else:
+            @pl.when(z < lines - 1)
+            def _():
+                line_copy(a, slot, piece, False).wait_send()
+        pair_copy(a, slot, piece).wait_send()
+        row_piece = piece_of(z, turn)
+        for gg in range(2):
+            way = (turn + gg) % 2
+            span = fwd * (1 - way) + bwd * way
+
+            @pl.when(span < planes - 1)
+            def _():
+                ring_copy(rbuf.at[a, slot, gg, row_piece], a, slot, gg, row_piece, way).wait_send()
+
+    def finish_step(k, carry):
+        each_slot(k, finish)
+        return carry
+
+    lax.fori_loop(0, 2 * planes * lines, finish_step, 0)
+    for out in outs:
+        out[...] = out[...] * norm_factor
+
+
+def fused(attn_input, mlp_input):
+    groups, tiles = lax.axis_size("grp"), lax.axis_size("tile")
+    tok, width = attn_input.shape
+    ct, rh = width // ROWB, width // ROWB // groups
+    norm_factor = 2.0 / (tok * tiles * groups)
+    dma = pltpu.SemaphoreType.DMA
+    cell = (2, ROWB, ROWB)
+    hess = pl.pallas_call(
+        functools.partial(kernel, norm_factor),
+        out_shape=[jax.ShapeDtypeStruct((rh, ct), jnp.float32)] * 2,
+        in_specs=[pl.BlockSpec(memory_space=pl.ANY)] * 2,
+        out_specs=[pl.BlockSpec(memory_space=pltpu.VMEM)] * 2,
+        scratch_shapes=[
+            pltpu.VMEM(cell + (tok, ct), jnp.bfloat16),
+            pltpu.VMEM(cell + (tok, ct), jnp.bfloat16),
+            pltpu.VMEM((2, ROWB, groups, ROWB, tok, rh), jnp.bfloat16),
+            dma(cell), dma(cell), dma((2, ROWB, groups, ROWB)),
+            dma((2, ROWB - 1)), dma(cell), dma(cell), dma(cell), dma((2, ROWB, groups, ROWB)),
+        ],
+        compiler_params=pltpu.CompilerParams(collective_id=0, has_side_effects=True, vmem_limit_bytes=48 * 1024 * 1024),
+    )(attn_input, mlp_input)
+    return hess[0][None], hess[1][None]
+
+
 def body(attn_input, mlp_input):
+    if lax.axis_size("grp") == 2 and lax.axis_size("tile") == ROWB * ROWB:
+        return fused(attn_input, mlp_input)
     return (hessian_share(attn_input), hessian_share(mlp_input))
 
 

time: 292 us -> 338 us (1.16); the launches traced: 290 us -> 331 us
  Pallas kernels: 0 us -> 326 us
  blocking collectives: 124 us -> 0 us
  waiting for transfers between devices: 97.7 us -> 0 us
  starting transfers between devices: 21.2 us -> 0 us
  matrix products: 17.4 us -> 0 us
  between operations: 14.1 us -> 0.65 us
  other arithmetic: 6.44 us -> 0 us
  local copies, waits for them, and re-layouts: 8.85 us -> 4.72 us
    pallas_call x0 -> x1, Pallas kernels: none -> 326 us  [fused(): pl.pallas_call(functools.partial(kernel, norm_factor), out_shape=[jax.Sha...]
    all_to_all x4 -> x0, blocking collectives: 124 us -> none  [accumulate(): lax.all_to_all(col_send, 'tile', split_axis=0, concat_axis=0, tiled=True)]
    all_to_all x4 -> x0, waiting for transfers between devices: 87 us -> none  [accumulate(): lax.all_to_all(row_send, 'tile', split_axis=0, concat_axis=0, tiled=True)]
    all_to_all x4 -> x0, starting transfers between devices: 21.1 us -> none  [accumulate(): lax.all_to_all(row_send, 'tile', split_axis=0, concat_axis=0, tiled=True)]
    dot_general x4 -> x0, matrix products: 17.4 us -> none  [accumulate(): lax.dot_general(rows_flat, cols_flat, (((0,), (0,)), ((), ())), preferred...]
    reduce_scatter x2 -> x0, waiting for transfers between devices: 10.7 us -> none  [tile_first(): lax.psum_scatter(partial_value, 'grp', scatter_dimension=0, tiled=True)]
    mul x2 -> x0, other arithmetic: 6.44 us -> none  [hessian_share(): return shares * norm_factor]
    broadcast_in_dim x4 -> x0, local copies, waits for them, and re-layouts: 4.4 us -> none  [accumulate(): row_send = jnp.repeat(row_parts, col_blocks, axis=0)]
  transfers between devices with their start and end apart: 6 -> 0, of which waited for: 5 -> 0; matrix products, arithmetic and copies ran while one was open for 5% -> 0% of each run, Pallas kernels for 0% -> 0%
where the time goes in v1:
time: 338 us; the launch traced here: 331 us
  Pallas kernels  326 us (96%)
  local copies, waits for them, and re-layouts  4.72 us (1%)
    pallas_call x1, Pallas kernels, fused(): pl.pallas_call(functools.partial(kernel, norm_factor), out_shape=[jax.Sha...  326 us

profile of v1, /device:TPU:2, one launch (start us, length us, event | category | flops | bytes accessed | tf_op | source)
XLA Modules:
  0.0 331.2 jit_solution(8164282535447437952)
XLA Ops:
  0.6 0.0 copy-start
  0.6 1.0 copy-done
  1.7 0.0 copy-start.1
  1.7 1.0 copy-done.1
  2.7 325.9 %shard_map.41 = (f32[512,1024]{1,0:T(8,128)S(1)}, f32[512,1024]{1,0:T(8,128)S(1)}) custom-call(bf16[64,4096]{1,0:T(8,128)(2,1)S(1)} %copy-done, bf16[64,4096]{1,0:T(8,128)(2,1)S(1)} %copy-done.1), custom_call_target="tpu_custom_call" | custom-call | tf_op jit(solution)/shard_map/pallas_call | solution.py:256
  328.6 1.3 copy.6
  329.9 1.3 copy.7
Async XLA Ops:
  0.6 1.0 copy-start
  1.7 1.0 copy-start.1

commit v2 on v1

--- a/solution.py
+++ b/solution.py
@@ -10,7 +10,8 @@
 ROWB = 4
 TOKB = 32
 MESH = pl.DeviceIdType.MESH
-LAG = 4
+HOP = 3
+LAG = 1 + HOP * (ROWB - 1)
 
 
 def tile_first(inputs, tile_count):
@@ -177,18 +178,19 @@
         landed(dbuf.at[a, slot, piece], d_recv.at[a, slot, piece])
         root_feed(dbuf.at[a, slot, piece, :, half], a, slot, 1 - g, piece, turn)
 
-    def row_phase(a, slot, turn, dist, from_high):
-        piece = piece_of(z, turn)
-        for step in range(2):
-            gg = g if step == 0 else 1 - g
+    def row_phase(way, span):
+        def action(a, slot, turn, dist, from_high):
+            piece = piece_of(z, turn)
+            gg = (turn + way) % 2
             landed(rbuf.at[a, slot, gg, piece], r_recv.at[a, slot, gg, piece])
-            way = (turn + gg) % 2
-            span = fwd * (1 - way) + bwd * way
 
             @pl.when((span > 0) & (span < planes - 1))
             def _():
                 ring_copy(rbuf.at[a, slot, gg, piece], a, slot, gg, piece, way).start()
 
+        return action
+
+    def multiply(a, slot, turn, dist, from_high):
         @pl.when(turn == planes - 1)
         def _():
             for arr in range(2):
@@ -204,7 +206,9 @@
     def step(k, carry):
         each_slot(k, col_phase)
         each_slot(k - 1, pair_phase)
-        each_slot(k - LAG, row_phase)
+        each_slot(k - 1 - HOP * jnp.where(fwd == 0, 1, fwd), row_phase(0, fwd))
+        each_slot(k - 1 - HOP * jnp.where(bwd == 0, 1, bwd), row_phase(1, bwd))
+        each_slot(k - LAG, multiply)
         return carry
 
     lax.fori_loop(0, 2 * planes * lines + LAG, step, 0)

time: 338 us -> 96.1 us (0.28); the launches traced: 331 us -> 95.8 us
  Pallas kernels: 326 us -> 90.5 us
    pallas_call x1, Pallas kernels: 326 us -> 90.5 us  [fused(): pl.pallas_call(functools.partial(kernel, norm_factor), out_shape=[jax.Sha...]
where the time goes in v2:
time: 96.1 us; the launch traced here: 95.8 us
  Pallas kernels  90.5 us (94%)
  local copies, waits for them, and re-layouts  4.72 us (5%)
    pallas_call x1, Pallas kernels, fused(): pl.pallas_call(functools.partial(kernel, norm_factor), out_shape=[jax.Sha...  90.5 us
    unnamed x6, local copies, waits for them, and re-layouts  4.72 us

profile of v2, /device:TPU:2, one launch (start us, length us, event | category | flops | bytes accessed | tf_op | source)
XLA Modules:
  0.0 95.8 jit_solution(4209241686777077189)
XLA Ops:
  0.6 0.0 copy-start
  0.6 1.0 %copy-done = bf16[64,4096]{1,0:T(8,128)(2,1)S(1)} copy-done((bf16[64,4096]{1,0:T(8,128)(2,1)S(1)}, bf16[64,4096]{1,0:T(8,128)(2,1)}, u32[]{:S(2)}) %copy-start) | copy-done | bytes 524312
  1.7 0.0 copy-start.1
  1.7 1.0 %copy-done.1 = bf16[64,4096]{1,0:T(8,128)(2,1)S(1)} copy-done((bf16[64,4096]{1,0:T(8,128)(2,1)S(1)}, bf16[64,4096]{1,0:T(8,128)(2,1)}, u32[]{:S(2)}) %copy-start.1) | copy-done | bytes 524312
  2.7 90.5 %shard_map.41 = (f32[512,1024]{1,0:T(8,128)S(1)}, f32[512,1024]{1,0:T(8,128)S(1)}) custom-call(bf16[64,4096]{1,0:T(8,128)(2,1)S(1)} %copy-done, bf16[64,4096]{1,0:T(8,128)(2,1)S(1)} %copy-done.1), custom_call_target="tpu_custom_call" | custom-call | tf_op jit(solution)/shard_map/pallas_call | solution.py:260
  93.2 1.3 %copy.6 = f32[1,512,1024]{2,1,0:T(8,128)} copy(f32[1,512,1024]{2,1,0:T(8,128)S(1)} %bitcast.3) | data formatting | bytes 4194304
  94.5 1.3 %copy.7 = f32[1,512,1024]{2,1,0:T(8,128)} copy(f32[1,512,1024]{2,1,0:T(8,128)S(1)} %bitcast.2) | data formatting | bytes 4194304
Async XLA Ops:
  0.6 1.0 %copy-start = (bf16[64,4096]{1,0:T(8,128)(2,1)S(1)}, bf16[64,4096]{1,0:T(8,128)(2,1)}, u32[]{:S(2)}) copy-start(bf16[64,4096]{1,0:T(8,128)(2,1)} %xa.1) | copy-start | bytes 1572868
  1.7 1.0 %copy-start.1 = (bf16[64,4096]{1,0:T(8,128)(2,1)S(1)}, bf16[64,4096]{1,0:T(8,128)(2,1)}, u32[]{:S(2)}) copy-start(bf16[64,4096]{1,0:T(8,128)(2,1)} %xm.1) | copy-start | bytes 1572868

commit v3 on v2

--- a/solution.py
+++ b/solution.py
@@ -1,5 +1,3 @@
-import functools
-
 import jax
 import jax.numpy as jnp
 from jax import lax
@@ -10,8 +8,8 @@
 ROWB = 4
 TOKB = 32
 MESH = pl.DeviceIdType.MESH
-HOP = 3
-LAG = 1 + HOP * (ROWB - 1)
+END_HOP = 2
+MID_HOP = 4
 
 
 def tile_first(inputs, tile_count):
@@ -61,7 +59,7 @@
     return jnp.where(turn == 0, home, jnp.where(turn == 1, near, jnp.where(turn == 2, far, ROWB - 1 - home)))
 
 
-def kernel(norm_factor, xa, xm, out_a, out_m, cbuf, dbuf, rbuf, c_recv, d_recv, r_recv, s1_send, dn_send, up_send, d_send, r_send):
+def kernel(xa, xm, out_a, out_m, cbuf, dbuf, rbuf, c_recv, d_recv, r_recv, s1_send, dn_send, up_send, d_send, r_send):
     lines = planes = ROWB
     g = lax.axis_index("grp")
     t = lax.axis_index("tile")
@@ -130,7 +128,8 @@
 
     for a in range(2):
         own_copy(a).start()
-        for turn in range(1, planes):
+    for turn in range(1, planes):
+        for a in range(2):
             s1_copy(a, turn).start()
     for out in outs:
         out[...] = jnp.zeros_like(out)
@@ -142,7 +141,7 @@
             ring_copy(src, a, slot, gg, piece, (turn + gg) % 2).start()
 
     def each_slot(k, action):
-        dist, a, turn = k // (2 * planes), (k // planes) % 2, k % planes
+        dist, turn, a = k // (2 * planes), (k // 2) % planes, k % 2
         high, low = z + dist, z - dist
 
         @pl.when((k >= 0) & (k < 2 * planes * lines))
@@ -203,15 +202,18 @@
                             cols[arr, slot].reshape(planes * tok, ct),
                             (((0,), (0,)), ((), ())), preferred_element_type=jnp.float32)
 
+    hop = jnp.where((z == 0) | (z == lines - 1), END_HOP, MID_HOP)
+    last = 1 + hop * (planes - 1)
+
     def step(k, carry):
         each_slot(k, col_phase)
         each_slot(k - 1, pair_phase)
-        each_slot(k - 1 - HOP * jnp.where(fwd == 0, 1, fwd), row_phase(0, fwd))
-        each_slot(k - 1 - HOP * jnp.where(bwd == 0, 1, bwd), row_phase(1, bwd))
-        each_slot(k - LAG, multiply)
+        each_slot(k - 1 - hop * jnp.where(fwd == 0, 1, fwd), row_phase(0, fwd))
+        each_slot(k - 1 - hop * jnp.where(bwd == 0, 1, bwd), row_phase(1, bwd))
+        each_slot(k - last, multiply)
         return carry
 
-    lax.fori_loop(0, 2 * planes * lines + LAG, step, 0)
+    lax.fori_loop(0, 2 * planes * lines + last, step, 0)
 
     for a in range(2):
         for turn in range(1, planes):
@@ -246,8 +248,6 @@
         return carry
 
     lax.fori_loop(0, 2 * planes * lines, finish_step, 0)
-    for out in outs:
-        out[...] = out[...] * norm_factor
 
 
 def fused(attn_input, mlp_input):
@@ -258,7 +258,7 @@
     dma = pltpu.SemaphoreType.DMA
     cell = (2, ROWB, ROWB)
     hess = pl.pallas_call(
-        functools.partial(kernel, norm_factor),
+        kernel,
         out_shape=[jax.ShapeDtypeStruct((rh, ct), jnp.float32)] * 2,
         in_specs=[pl.BlockSpec(memory_space=pl.ANY)] * 2,
         out_specs=[pl.BlockSpec(memory_space=pltpu.VMEM)] * 2,
@@ -271,7 +271,7 @@
         ],
         compiler_params=pltpu.CompilerParams(collective_id=0, has_side_effects=True, vmem_limit_bytes=48 * 1024 * 1024),
     )(attn_input, mlp_input)
-    return hess[0][None], hess[1][None]
+    return hess[0][None] * norm_factor, hess[1][None] * norm_factor
 
 
 def body(attn_input, mlp_input):

time: 96.1 us -> 94.7 us (0.985)
  other arithmetic: 0 us -> 2.85 us
  local copies, waits for them, and re-layouts: 4.72 us -> 2.08 us
  Pallas kernels: 90.5 us -> 88.9 us
    mul x0 -> x1, other arithmetic: none -> 2.85 us  [fused(): return (hess[0][None] * norm_factor, hess[1][None] * norm_factor)]
    unnamed x6 -> x4, local copies, waits for them, and re-layouts: 4.72 us -> 2.08 us
    pallas_call x1, Pallas kernels: 90.5 us -> 88.9 us  [fused(): pl.pallas_call(kernel, out_shape=[jax.ShapeDtypeStruct((rh, ct), jnp.floa...]
where the time goes in v3:
time: 94.7 us; the launch traced here: 94.4 us
  Pallas kernels  88.9 us (94%)
  other arithmetic  2.85 us (3%)
  local copies, waits for them, and re-layouts  2.08 us (2%)
    pallas_call x1, Pallas kernels, fused(): pl.pallas_call(kernel, out_shape=[jax.ShapeDtypeStruct((rh, ct), jnp.floa...  88.9 us
    mul x1, other arithmetic, fused(): return (hess[0][None] * norm_factor, hess[1][None] * norm_factor)  2.85 us
    unnamed x4, local copies, waits for them, and re-layouts  2.08 us

profile of v3, /device:TPU:2, one launch (start us, length us, event | category | flops | bytes accessed | tf_op | source)
XLA Modules:
  0.0 94.4 jit_solution(15932997600308177860)
XLA Ops:
  0.6 0.0 copy-start
  0.6 1.0 %copy-done = bf16[64,4096]{1,0:T(8,128)(2,1)S(1)} copy-done((bf16[64,4096]{1,0:T(8,128)(2,1)S(1)}, bf16[64,4096]{1,0:T(8,128)(2,1)}, u32[]{:S(2)}) %copy-start) | copy-done | bytes 524312
  1.7 0.0 copy-start.1
  1.7 1.0 %copy-done.1 = bf16[64,4096]{1,0:T(8,128)(2,1)S(1)} copy-done((bf16[64,4096]{1,0:T(8,128)(2,1)S(1)}, bf16[64,4096]{1,0:T(8,128)(2,1)}, u32[]{:S(2)}) %copy-start.1) | copy-done | bytes 524312
  2.7 88.9 %shard_map.41 = (f32[512,1024]{1,0:T(8,128)S(1)}, f32[512,1024]{1,0:T(8,128)S(1)}) custom-call(bf16[64,4096]{1,0:T(8,128)(2,1)S(1)} %copy-done, bf16[64,4096]{1,0:T(8,128)(2,1)S(1)} %copy-done.1), custom_call_target="tpu_custom_call" | custom-call | tf_op jit(solution)/shard_map/pallas_call | solution.py:260
  91.6 2.9 %multiply_bitcast_fusion = (f32[1,512,1024]{2,1,0:T(8,128)}, f32[1,512,1024]{2,1,0:T(8,128)}) fusion(f32[512,1024]{1,0:T(8,128)S(1)} %get-tuple-element.5, f32[512,1024]{1,0:T(8,128)S(1)} %get-tuple-element.4), kind=kLoop, calls=%fused_computation | loop fusion | flops 1048576 | bytes 8388608 | tf_op jit(solution)/shard_map/mul | solution.py:274
Async XLA Ops:
  0.6 1.0 %copy-start = (bf16[64,4096]{1,0:T(8,128)(2,1)S(1)}, bf16[64,4096]{1,0:T(8,128)(2,1)}, u32[]{:S(2)}) copy-start(bf16[64,4096]{1,0:T(8,128)(2,1)} %xa.1) | copy-start | bytes 1572868
  1.7 1.0 %copy-start.1 = (bf16[64,4096]{1,0:T(8,128)(2,1)S(1)}, bf16[64,4096]{1,0:T(8,128)(2,1)}, u32[]{:S(2)}) copy-start(bf16[64,4096]{1,0:T(8,128)(2,1)} %xm.1) | copy-start | bytes 1572868
